TPU v7x, 32 devices: a whole 2x2x4 slice. The times are simulated.
32 devices in a mesh: blk: 16 (over z, x, core), rep: 2 (over y).
Axes of the slice: x: 2, y: 2, z: 4, core: 2. Of those that a mesh axis runs over, the one named last changes fastest.
Arguments:
- prices: float32 [512], replicated, may hold values from 0.5 to 1.5
- capacity: float32 [512], replicated, may hold values from -8 to 8
- coupling: bfloat16 [48, 32, 512], P(None, 'blk', 'rep'), may hold values from -0.25 to 0.25
- assign: int32 [65536], P(('blk', 'rep')), may hold values from 0 to 31
- avail: int32 [48, 65536], P(None, ('blk', 'rep')), may hold values 0 or 1
- agent_cap: float32 [65536], P(('blk', 'rep')), may hold values from 0.5 to 2
- value: float32 [48, 65536], P(None, ('blk', 'rep')), may hold values from -6 to 6
- weight: float32 [48, 65536], P(None, ('blk', 'rep')), may hold values from 0.5 to 2
- warm: float32 [48, 65536], P(None, ('blk', 'rep')), may hold values from 0 to 2
Outputs:
- plan: float32 [48, 65536], P(None, ('blk', 'rep'))
- new_prices: float32 [512], replicated
All inputs are finite; a program needn't handle non-finite values. No bound on the sum of `avail` on one device may be relied on, other than what follows from the above.
Results may differ from a plain program's by a relative error of at most 0.0003.
Values may be sent and summed in bfloat16 or wider, within the bound.
A program may use at most 64 MiB of HBM per device.

v0:
```python
import jax
import jax.numpy as jnp
from jax import lax
from jax.sharding import PartitionSpec as P

INNER = 8


def smooth_of(plan_now):
    diffs = plan_now[1:] - plan_now[:-1]
    zero_row = jnp.zeros((1, plan_now.shape[1]), jnp.float32)
    return jnp.concatenate([zero_row, diffs], 0) - jnp.concatenate([diffs, zero_row], 0)


def price_block(slab_part, lam_half):
    return jnp.einsum(
        "tfr,r->tf", slab_part.astype(jnp.float32), lam_half, precision=lax.Precision.HIGHEST
    )


def sum_block(slab_part, load_part):
    return jnp.einsum(
        "tfr,tf->r", slab_part.astype(jnp.float32), load_part, precision=lax.Precision.HIGHEST
    )


def shards(prices, capacity, coupling, assign, avail, agent_cap, value, weight, warm):
    feed_local = coupling.shape[1]
    half_rows = coupling.shape[2]
    feeders = feed_local * lax.axis_size("blk")
    total_agents = warm.shape[1] * lax.axis_size("blk") * lax.axis_size("rep")
    row_start = lax.axis_index("rep") * half_rows
    lam_half = lax.dynamic_slice_in_dim(prices, row_start, half_rows, 0)
    onehot = (assign[None, :] == lax.iota(jnp.int32, feeders)[:, None]).astype(jnp.float32)
    half_table = price_block(lax.all_gather(coupling, "blk", axis=1, tiled=True), lam_half)
    table = lax.psum(half_table, "rep")
    price = jnp.dot(table, onehot, precision=lax.Precision.HIGHEST)
    upper = agent_cap[None, :] * avail.astype(jnp.float32)
    plan = jnp.clip(warm, 0.0, upper)
    for _ in range(INNER):
        gradient = weight * plan + 1.0 * smooth_of(plan) - value + price
        plan = jnp.clip(plan - 0.15 * gradient, 0.0, upper)
    local_loads = lax.dot_general(
        plan, onehot, (((1,), (1,)), ((), ())), precision=lax.Precision.HIGHEST
    )
    local_loads = local_loads * (feeders / total_agents)
    pair_loads = lax.psum(local_loads.astype(jnp.bfloat16), "rep").astype(jnp.float32)
    half_sums = sum_block(lax.all_gather(coupling, "blk", axis=1, tiled=True), pair_loads)
    placed = lax.dynamic_update_slice_in_dim(
        jnp.zeros(prices.shape, jnp.float32), half_sums, row_start, 0
    )
    sums = lax.psum(placed, ("blk", "rep"))
    new_prices = jnp.maximum(0.0, prices + 0.1 * (sums - capacity))
    return (plan, new_prices)


def solution(mesh):
    placed = (
        P(),
        P(),
        P(None, "blk", "rep"),
        P(("blk", "rep")),
        P(None, ("blk", "rep")),
        P(("blk", "rep")),
        P(None, ("blk", "rep")),
        P(None, ("blk", "rep")),
        P(None, ("blk", "rep")),
    )
    return jax.shard_map(
        shards,
        mesh=mesh,
        in_specs=placed,
        out_specs=(P(None, ("blk", "rep")), P()),
        check_vma=False,
    )
```

profile of v0, /device:TPU:14, one launch (start us, length us, event | category | flops | bytes accessed | tf_op | source)
XLA Modules:
  0.0 87.3 jit_solution(13477924110720840931)
XLA Ops:
  0.6 0.0 copy-start.7
  0.6 0.7 copy-done.7
  1.3 0.1 dynamic_slice.3
  1.4 0.8 copy.11
  2.2 17.3 %all_gather.4 = bf16[48,32,256]{2,0,1:T(8,128)(2,1)S(1)} all-gather(bf16[48,2,256]{2,0,1:T(8,128)(2,1)S(1)} %copy.11), channel_id=1, replica_groups=mesh['blk'=16,'rep'=2] {'blk'}, dimensions={1}, use_global_device_ids=true | all-gather | bytes 835584 | tf_op jit(solution)/shard_map/all_gather | solution.py:35
  19.5 0.0 copy-start
  19.5 0.0 copy-start.4
  19.5 1.2 %fusion.4 = f32[1,48,32]{1,0,2:T(1,128)S(1)} fusion(f32[256,1,1]{0,1,2:T(1,128)S(1)} %bitcast.12, bf16[48,32,256]{2,0,1:T(8,128)(2,1)S(1)} %all_gather.4), kind=kOutput, calls=%fused_computation.25 | convolution fusion | flops 4718592 | bytes 793600 | tf_op jit(solution)/shard_map/tfr,r->tf/dot_general | solution.py:16
  20.7 0.1 copy.12
  20.8 0.0 copy-start.5
  20.8 7.4 %psum.21 = f32[48,32]{1,0:T(8,128)S(1)} all-reduce(f32[48,32]{1,0:T(8,128)S(1)} %bitcast.10), channel_id=1, replica_groups=mesh['blk'=16,'rep'=2] {'rep'}, use_global_device_ids=true, to_apply=%region_0.0 | all-reduce | flops 1536 | bytes 12288 | tf_op jit(solution)/shard_map/psum | solution.py:36
  28.3 0.0 copy-done
  28.3 0.0 copy-done.4
  28.3 0.0 copy-done.5
  28.3 0.1 maximum_minimum_fusion.8
  28.4 0.0 copy-start.1
  28.4 0.0 copy-start.2
  28.4 0.0 copy-start.6
  28.4 0.9 %copy-done.1 = f32[48,2048]{1,0:T(8,128)S(1)} copy-done((f32[48,2048]{1,0:T(8,128)S(1)}, f32[48,2048]{1,0:T(8,128)}, u32[]{:S(2)}) %copy-start.1) | copy-done | bytes 393240
  29.4 0.1 copy-done.2
  29.5 0.0 copy-done.6
  29.5 0.5 maximum_minimum_fusion.7
  30.0 0.2 maximum_minimum_fusion.6
  30.3 0.3 maximum_minimum_fusion.5
  30.6 0.2 maximum_minimum_fusion.4
  30.9 0.3 maximum_minimum_fusion.3
  31.3 0.2 maximum_minimum_fusion.2
  31.5 0.3 maximum_minimum_fusion.1
  31.9 0.2 maximum_minimum_fusion
  32.1 0.0 copy-start.3
  32.1 0.3 fusion
  32.5 8.1 %psum.22 = bf16[48,32]{1,0:T(8,128)(2,1)S(1)} all-reduce(bf16[48,32]{1,0:T(8,128)(2,1)S(1)} %fusion), channel_id=1, replica_groups=mesh['blk'=16,'rep'=2] {'rep'}, use_global_device_ids=true, to_apply=%region_1.2 | all-reduce | flops 1536 | bytes 6144 | tf_op jit(solution)/shard_map/psum | solution.py:47
  40.6 0.1 copy.13
  40.7 0.3 fusion.5
  41.0 0.0 copy-done.3
  41.0 0.2 dynamic_update_slice.3
  41.2 0.0 copy-start.8
  41.2 45.5 %psum.23 = f32[512]{0:T(512)S(1)} all-reduce(f32[512]{0:T(512)S(1)} %dynamic_update_slice.3), channel_id=1, replica_groups=mesh['blk'=16,'rep'=2] {'blk','rep'}, use_global_device_ids=true, to_apply=%region_2.3 | all-reduce | flops 512 | bytes 4096 | tf_op jit(solution)/shard_map/psum | solution.py:52
  86.7 0.0 copy-done.8
  86.7 0.6 add_maximum_fusion
  (9 shorter events, 0.3 us)
Async XLA Ops:
  0.6 0.7 copy-start.7
  19.5 8.7 %copy-start = (s32[48,2048]{1,0:T(8,128)S(1)}, s32[48,2048]{1,0:T(8,128)}, u32[]{:S(2)}) copy-start(s32[48,2048]{1,0:T(8,128)} %param.13) | copy-start | bytes 1179652
  19.5 8.7 %copy-start.4 = (f32[48,2048]{1,0:T(8,128)S(1)}, f32[48,2048]{1,0:T(8,128)}, u32[]{:S(2)}) copy-start(f32[48,2048]{1,0:T(8,128)} %param.17) | copy-start | bytes 1179652
  20.8 7.5 %copy-start.5 = (f32[2048]{0:T(1024)S(1)}, f32[2048]{0:T(1024)}, u32[]{:S(2)}) copy-start(f32[2048]{0:T(1024)} %param.14) | copy-start | bytes 24580
  28.4 1.0 %copy-start.1 = (f32[48,2048]{1,0:T(8,128)S(1)}, f32[48,2048]{1,0:T(8,128)}, u32[]{:S(2)}) copy-start(f32[48,2048]{1,0:T(8,128)} %param.15) | copy-start | bytes 1179652
  28.4 1.1 %copy-start.2 = (f32[48,2048]{1,0:T(8,128)S(1)}, f32[48,2048]{1,0:T(8,128)}, u32[]{:S(2)}) copy-start(f32[48,2048]{1,0:T(8,128)} %param.16) | copy-start | bytes 1179652
  28.4 1.1 %copy-start.6 = (s32[2048]{0:T(1024)S(1)}, s32[2048]{0:T(1024)}, u32[]{:S(2)}) copy-start(s32[2048]{0:T(1024)} %param.12) | copy-start | bytes 24580
  32.1 8.8 %copy-start.3 = (f32[48,2048]{1,0:T(8,128)}, f32[48,2048]{1,0:T(8,128)S(1)}, u32[]{:S(2)}) copy-start(f32[48,2048]{1,0:T(8,128)S(1)} %maximum_minimum_fusion) | copy-start | bytes 1179652
  41.2 45.5 %copy-start.8 = (f32[512]{0:T(512)S(1)}, f32[512]{0:T(512)}, u32[]{:S(2)}) copy-start(f32[512]{0:T(512)} %param.10) | copy-start | bytes 6148
where the time goes:
time: 87.7 us; the launch traced here: 87.3 us
  blocking collectives  78.4 us (89%)
  local copies, waits for them, and re-layouts  3.02 us (3%)
  other arithmetic  2.8 us (3%)
  matrix products  2.29 us (3%)
    psum x1, blocking collectives, shards(): sums = lax.psum(placed, ('blk', 'rep'))  45.5 us
    all_gather x1, blocking collectives, shards(): lax.all_gather(coupling, 'blk', axis=1, tiled=True)  17.3 us
    psum x1, blocking collectives, shards(): lax.psum(local_loads.astype(jnp.bfloat16), 'rep').astype(jnp.float32)  8.11 us
    psum x1, blocking collectives, shards(): table = lax.psum(half_table, 'rep')  7.44 us
    unnamed x19, local copies, waits for them, and re-layouts  2.55 us
    min x7, other arithmetic, shards(): plan = jnp.clip(plan - 0.15 * gradient, 0.0, upper)  1.82 us

commit v1 on v0

--- a/solution.py
+++ b/solution.py
@@ -33,7 +33,8 @@
     lam_half = lax.dynamic_slice_in_dim(prices, row_start, half_rows, 0)
     onehot = (assign[None, :] == lax.iota(jnp.int32, feeders)[:, None]).astype(jnp.float32)
     half_table = price_block(lax.all_gather(coupling, "blk", axis=1, tiled=True), lam_half)
-    table = lax.psum(half_table, "rep")
+    parts = lax.all_gather(half_table, "rep")
+    table = jnp.sum(parts, axis=0)
     price = jnp.dot(table, onehot, precision=lax.Precision.HIGHEST)
     upper = agent_cap[None, :] * avail.astype(jnp.float32)
     plan = jnp.clip(warm, 0.0, upper)

time: 87.7 us -> 82.1 us (0.936)
  blocking collectives: 78.4 us -> 72.3 us
    psum x1 -> x0, blocking collectives: 7.44 us -> none  [shards(): table = lax.psum(half_table, 'rep')]
    all_gather x0 -> x1, blocking collectives: none -> 4.41 us  [shards(): parts = lax.all_gather(half_table, 'rep')]
    psum x1, blocking collectives: 8.11 us -> 5.02 us  [shards(): lax.psum(local_loads.astype(jnp.bfloat16), 'rep').astype(jnp.float32)]
where the time goes in v1:
time: 82.1 us; the launch traced here: 81.7 us
  blocking collectives  72.3 us (88%)
  local copies, waits for them, and re-layouts  3.52 us (4%)
  other arithmetic  2.8 us (3%)
  matrix products  2.34 us (3%)
    psum x1, blocking collectives, shards(): sums = lax.psum(placed, ('blk', 'rep'))  45.5 us
    all_gather x1, blocking collectives, shards(): lax.all_gather(coupling, 'blk', axis=1, tiled=True)  17.3 us
    psum x1, blocking collectives, shards(): lax.psum(local_loads.astype(jnp.bfloat16), 'rep').astype(jnp.float32)  5.02 us
    all_gather x1, blocking collectives, shards(): parts = lax.all_gather(half_table, 'rep')  4.41 us
    unnamed x19, local copies, waits for them, and re-layouts  3.21 us
    min x7, other arithmetic, shards(): plan = jnp.clip(plan - 0.15 * gradient, 0.0, upper)  1.82 us

profile of v1, /device:TPU:14, one launch (start us, length us, event | category | flops | bytes accessed | tf_op | source)
XLA Modules:
  0.0 81.7 jit_solution(5159544722315443330)
XLA Ops:
  0.6 0.0 copy-start.7
  0.6 0.7 copy-done.7
  1.3 0.1 dynamic_slice.3
  1.4 0.8 copy.12
  2.2 17.3 %all_gather.10 = bf16[48,32,256]{2,0,1:T(8,128)(2,1)S(1)} all-gather(bf16[48,2,256]{2,0,1:T(8,128)(2,1)S(1)} %copy.12), channel_id=1, replica_groups=mesh['blk'=16,'rep'=2] {'blk'}, dimensions={1}, use_global_device_ids=true | all-gather | bytes 835584 | tf_op jit(solution)/shard_map/all_gather | solution.py:35
  19.5 0.0 copy-start
  19.5 0.0 copy-start.4
  19.5 1.2 %fusion.6 = f32[1,48,32]{1,0,2:T(1,128)S(1)} fusion(f32[256,1,1]{0,1,2:T(1,128)S(1)} %bitcast.12, bf16[48,32,256]{2,0,1:T(8,128)(2,1)S(1)} %all_gather.10), kind=kOutput, calls=%fused_computation.27 | convolution fusion | flops 4718592 | bytes 793600 | tf_op jit(solution)/shard_map/tfr,r->tf/dot_general | solution.py:16
  20.7 4.4 %all-gather.1 = f32[2,48,32]{1,2,0:T(8,128)S(1)} all-gather(f32[1,48,32]{1,2,0:T(8,128)S(1)} %bitcast.10), channel_id=2, replica_groups=mesh['blk'=16,'rep'=2] {'rep'}, dimensions={0}, use_global_device_ids=true | all-gather | bytes 18432 | tf_op jit(solution)/shard_map/all_gather | solution.py:36
  25.2 0.0 copy-start.5
  25.2 0.0 copy-done
  25.2 0.0 copy-done.4
  25.2 0.7 copy-done.5
  25.9 0.1 maximum_minimum_fusion.8
  25.9 0.0 copy-start.1
  25.9 0.0 copy-start.2
  25.9 0.0 copy-start.6
  26.0 0.9 %copy-done.1 = f32[48,2048]{1,0:T(8,128)S(1)} copy-done((f32[48,2048]{1,0:T(8,128)S(1)}, f32[48,2048]{1,0:T(8,128)}, u32[]{:S(2)}) %copy-start.1) | copy-done | bytes 393240
  26.9 0.1 copy-done.2
  27.0 0.0 copy-done.6
  27.0 0.5 maximum_minimum_fusion.7
  27.6 0.2 maximum_minimum_fusion.6
  27.9 0.3 maximum_minimum_fusion.5
  28.3 0.2 maximum_minimum_fusion.4
  28.5 0.3 maximum_minimum_fusion.3
  28.9 0.2 maximum_minimum_fusion.2
  29.2 0.3 maximum_minimum_fusion.1
  29.5 0.2 maximum_minimum_fusion
  29.8 0.0 copy-start.3
  29.8 0.3 fusion
  30.1 5.0 %psum.14 = bf16[48,32]{0,1:T(8,128)(2,1)S(1)} all-reduce(bf16[48,32]{0,1:T(8,128)(2,1)S(1)} %fusion), channel_id=1, replica_groups=mesh['blk'=16,'rep'=2] {'rep'}, use_global_device_ids=true, to_apply=%region_1.2 | all-reduce | flops 1536 | bytes 6144 | tf_op jit(solution)/shard_map/psum | solution.py:48
  35.1 0.3 fusion.4
  35.4 0.0 copy-done.3
  35.4 0.2 dynamic_update_slice.3
  35.6 0.0 copy-start.8
  35.6 45.5 %psum.15 = f32[512]{0:T(512)S(1)} all-reduce(f32[512]{0:T(512)S(1)} %dynamic_update_slice.3), channel_id=1, replica_groups=mesh['blk'=16,'rep'=2] {'blk','rep'}, use_global_device_ids=true, to_apply=%region_2.3 | all-reduce | flops 512 | bytes 4096 | tf_op jit(solution)/shard_map/psum | solution.py:53
  81.2 0.0 copy-done.8
  81.2 0.6 add_maximum_fusion
  (10 shorter events, 0.3 us)
Async XLA Ops:
  0.6 0.7 copy-start.7
  19.5 5.6 %copy-start = (s32[48,2048]{1,0:T(8,128)S(1)}, s32[48,2048]{1,0:T(8,128)}, u32[]{:S(2)}) copy-start(s32[48,2048]{1,0:T(8,128)} %param.13) | copy-start | bytes 1179652
  19.5 5.7 %copy-start.4 = (f32[48,2048]{1,0:T(8,128)S(1)}, f32[48,2048]{1,0:T(8,128)}, u32[]{:S(2)}) copy-start(f32[48,2048]{1,0:T(8,128)} %param.17) | copy-start | bytes 1179652
  25.2 0.7 copy-start.5
  25.9 1.0 %copy-start.1 = (f32[48,2048]{1,0:T(8,128)S(1)}, f32[48,2048]{1,0:T(8,128)}, u32[]{:S(2)}) copy-start(f32[48,2048]{1,0:T(8,128)} %param.15) | copy-start | bytes 1179652
  25.9 1.1 %copy-start.2 = (f32[48,2048]{1,0:T(8,128)S(1)}, f32[48,2048]{1,0:T(8,128)}, u32[]{:S(2)}) copy-start(f32[48,2048]{1,0:T(8,128)} %param.16) | copy-start | bytes 1179652
  25.9 1.1 %copy-start.6 = (s32[2048]{0:T(1024)S(1)}, s32[2048]{0:T(1024)}, u32[]{:S(2)}) copy-start(s32[2048]{0:T(1024)} %param.12) | copy-start | bytes 24580
  29.8 5.7 %copy-start.3 = (f32[48,2048]{1,0:T(8,128)}, f32[48,2048]{1,0:T(8,128)S(1)}, u32[]{:S(2)}) copy-start(f32[48,2048]{1,0:T(8,128)S(1)} %maximum_minimum_fusion) | copy-start | bytes 1179652
  35.6 45.5 %copy-start.8 = (f32[512]{0:T(512)S(1)}, f32[512]{0:T(512)}, u32[]{:S(2)}) copy-start(f32[512]{0:T(512)} %param.10) | copy-start | bytes 6148
